TPU v7x, 32 devices: a whole 2x2x4 slice. The times are simulated.
32 devices in a mesh: groups: 2 (over y), seq: 16 (over z, x, core).
Axes of the slice: x: 2, y: 2, z: 4, core: 2. Of those that a mesh axis runs over, the one named last changes fastest.
Arguments:
- queries: bfloat16 [8192, 768], P(('groups', 'seq')), parts along dimension 0, may hold values from -30 to 30
- keys: bfloat16 [8192, 128], P(('groups', 'seq')), parts along dimension 0, may hold values from -14 to 14
- values: bfloat16 [8192, 128], P(('groups', 'seq')), parts along dimension 0, may hold values from -6 to 6
- span_ids: int32 [64], P(('groups', 'seq')), parts along dimension 0, may hold values from 0 to 31, each once
- lengths: int32 [16], P('groups'), parts along dimension 0, may hold values from 1 to 16, 32 in all
- page_dest: int32 [64], P('groups'), parts along dimension 0, may hold values from 0 to 31, each once
Outputs:
- context: bfloat16 [8192, 768], P(('groups', 'seq')), parts along dimension 0
- paged_kv: bfloat16 [64, 128, 256], P(('groups', 'seq')), parts along dimension 0
There are 2 independent parts, one for each index of `groups`. A program takes and returns all parts, laid end to end along the dimension named above; each array names one. Nothing has to cross between parts.
Inputs may be any that keep to these rules, and one draw needn't show every extreme that they name: `span_ids`: every packed span number appears once over the whole array. The lengths sum to 32, and one of them equals 16. `page_dest`: every page slot receives exactly one span.
All inputs are finite; a program needn't handle non-finite values.
Results may differ from a plain program's by a relative error of at most 0.012.
The roundings to bfloat16 on the way count: a program that leaves them out, or rounds other values in their place, can miss the bound.
Values may be sent and summed in bfloat16 or wider, within the bound.
A program may use at most 128 MiB of HBM per device.

v0:
```python
import math

import jax
import jax.numpy as jnp
from jax import lax
from jax.sharding import PartitionSpec as P

HD = 128
QH = 6
SPAN = 128


THETA = 1000000.0
NEG = -1e30


def rotate(x, pos):
    half = HD // 2
    freq = THETA ** (-(jnp.arange(half, dtype=jnp.float32) * 2.0 / HD))
    angle = pos[:, None] * freq[None, :]
    cosine = jnp.cos(angle)[:, None, :]
    sine = jnp.sin(angle)[:, None, :]
    first = x[..., :half]
    second = x[..., half:]
    return jnp.concatenate(
        [first * cosine - second * sine, second * cosine + first * sine], axis=-1
    )


def locate(tokens, lengths):
    span_of = tokens // SPAN
    ends = jnp.cumsum(lengths)
    start_span = jnp.sum(jnp.where(ends[None, :] <= span_of[:, None], lengths[None, :], 0), axis=1)
    start = start_span * SPAN
    return (start, tokens - start)


def attend(state, q_rows, query_tok, query_start, kv_block, tok_block, live):
    best, total, accum = state
    scores = jnp.dot(q_rows, kv_block[:, :HD].T, preferred_element_type=jnp.float32) * (
        1.0 / math.sqrt(HD)
    )
    mask = (
        live[None, :]
        & (tok_block[None, :] <= query_tok[:, None])
        & (tok_block[None, :] >= query_start[:, None])
    )
    fresh = jnp.maximum(best, jnp.max(jnp.where(mask, scores, NEG), axis=1))
    weights = jnp.where(mask, jnp.exp(scores - fresh[:, None]), 0.0)
    factor = jnp.exp(best - fresh)
    total = total * factor + jnp.sum(weights, axis=1)
    accum = accum * factor[:, None] + jnp.dot(
        weights.astype(jnp.bfloat16), kv_block[:, HD:], preferred_element_type=jnp.float32
    )
    return (fresh, total, accum)


def sweep(state, q_rows, query_tok, query_start, kv_rows, tok_rows, live):
    count = kv_rows.shape[0]
    width = math.gcd(count, 1024)
    blocks = count // width
    items = (
        kv_rows.reshape(blocks, width, kv_rows.shape[1]),
        tok_rows.reshape(blocks, width),
        live.reshape(blocks, width),
    )

    def advance(carry, item):
        return (attend(carry, q_rows, query_tok, query_start, item[0], item[1], item[2]), None)

    state, _ = lax.scan(advance, state, items)
    return state


def blank_state(rows):
    return (
        jnp.full((rows,), NEG, jnp.float32),
        jnp.zeros((rows,), jnp.float32),
        jnp.zeros((rows, HD), jnp.float32),
    )


def on_device(queries, keys, values, span_ids, lengths, page_dest):
    tok_dev = queries.shape[0]
    per_rank = span_ids.shape[0]
    span_total = page_dest.shape[0]
    offsets = jnp.arange(SPAN, dtype=jnp.int32)
    tokens = (span_ids[:, None] * SPAN + offsets[None, :]).reshape(-1)
    start, pos = locate(tokens, lengths)
    posf = pos.astype(jnp.float32)
    q_rot = (
        rotate(queries.astype(jnp.float32).reshape(tok_dev, QH, HD), posf)
        .astype(jnp.bfloat16)
        .reshape(tok_dev * QH, HD)
    )
    k_rot = rotate(keys.astype(jnp.float32)[:, None, :], posf)[:, 0, :].astype(jnp.bfloat16)
    packed = jnp.concatenate([k_rot, values], axis=1)
    query_tok = jnp.repeat(tokens, QH)
    query_start = jnp.repeat(start, QH)
    rank_base = lax.axis_index("seq") * per_rank
    wanted = rank_base + jnp.arange(per_rank, dtype=jnp.int32)
    span_range = jnp.arange(span_total, dtype=jnp.int32)
    page_span = jnp.sum(
        jnp.where(page_dest[None, :] == wanted[:, None], span_range[None, :], 0), axis=1
    )
    whole_kv, whole_tok = (
        lax.all_gather(packed, "seq", axis=0, tiled=True),
        lax.all_gather(tokens, "seq", axis=0, tiled=True),
    )
    owners = whole_tok.reshape(span_total, SPAN)[:, 0] // SPAN
    where_is = jnp.sum(
        jnp.where(owners[None, :] == span_range[:, None], span_range[None, :], 0), axis=1
    )
    reach = span_total // 2
    by_span = whole_kv.reshape(span_total, SPAN, 2 * HD)
    totals = []
    accums = []
    for slot in range(per_rank):
        window = span_ids[slot] - reach + 1 + jnp.arange(reach, dtype=jnp.int32)
        kv_rows = by_span[where_is[jnp.maximum(window, 0)]].reshape(reach * SPAN, 2 * HD)
        tok_rows = (window[:, None] * SPAN + offsets[None, :]).reshape(-1)
        live = jnp.repeat(window >= 0, SPAN)
        low = slot * SPAN * QH
        high = low + SPAN * QH
        result = sweep(
            blank_state(SPAN * QH),
            q_rot[low:high],
            query_tok[low:high],
            query_start[low:high],
            kv_rows,
            tok_rows,
            live,
        )
        totals.append(result[1])
        accums.append(result[2])
    total = jnp.concatenate(totals, axis=0)
    accum = jnp.concatenate(accums, axis=0)
    heads = whole_tok.reshape(-1, SPAN)[:, 0] // SPAN
    hit = (heads[None, :] == page_span[:, None]).astype(jnp.bfloat16)
    collected = jnp.dot(
        hit, whole_kv.reshape(heads.shape[0], SPAN * 2 * HD), preferred_element_type=jnp.float32
    )
    context = (accum / total[:, None]).astype(jnp.bfloat16).reshape(tok_dev, QH * HD)
    paged = collected.astype(jnp.bfloat16)
    return (context, paged.reshape(per_rank, SPAN, 2 * HD))


def solution(mesh):
    return jax.shard_map(
        on_device,
        mesh=mesh,
        in_specs=(
            P(("groups", "seq"), None),
            P(("groups", "seq"), None),
            P(("groups", "seq"), None),
            P(("groups", "seq")),
            P("groups"),
            P("groups"),
        ),
        out_specs=(P(("groups", "seq"), None), P(("groups", "seq"), None, None)),
        check_vma=False,
    )
```

profile of v0, /device:TPU:1, one launch (start us, length us, event | category | flops | bytes accessed | tf_op | source)
XLA Modules:
  0.0 130.1 jit_solution(4056476347390937415)
XLA Ops:
  18.3 23.0 %all-gather = s32[16,1,256]{2,1,0:T(1,128)S(1)} all-gather(s32[1,1,256]{2,1,0:T(1,128)S(1)} %bitcast.147), channel_id=1, replica_groups=mesh['groups'=2,'seq'=16] {'seq'}, dimensions={0}, use_global_device_ids=true | all-gather | bytes 17408 | tf_op jit(solution)/shard_map/all_gather | solution.py:108
  46.2 10.0 %all-gather.3.cloned.1.call-done = bf16[4096,256]{0,1:T(8,128)(2,1)} async-done(((bf16[256,256]{0,1:T(8,128)(2,1)}), bf16[4096,256]{0,1:T(8,128)(2,1)}) %all-gather.3.cloned.1.call-update) | async-done | bytes 2097168 | tf_op jit(solution)/shard_map/all_gather | solution.py:107
  56.3 3.3 %copy.53 = bf16[4096,256]{1,0:T(8,128)(2,1)S(1)} copy(bf16[4096,256]{0,1:T(8,128)(2,1)} %all-gather.3.cloned.1.call-done) | data formatting | bytes 4194304 | tf_op jit(solution)/shard_map/reshape | solution.py:115
  59.5 2.7 %reshape.328 = bf16[32,32768]{1,0:T(8,128)(2,1)} reshape(bf16[4096,256]{1,0:T(8,128)(2,1)S(1)} %copy.53) | data formatting | bytes 4194304 | tf_op jit(solution)/shard_map/reshape | solution.py:141
  63.8 18.1 %while.30 = (s32[]{:T(128)}, f32[768]{0:T(1024)S(1)}, f32[768]{0:T(1024)S(1)}, f32[768,128]{1,0:T(8,128)}, pred[2,1024]{1,0:T(4,128)(4,1)S(1)}, /*index=5*/s32[2...) while((s32[]{:T(128)}, f32[768]{0:T(1024)S(1)}, ...), condition=%wide.region_6.7_spmd.clone, body=%wide.region_3.6_spmd.clone.sunk | while | flops 421039872 | bytes 17352928 | solution.py:71
  63.9 1.9 %dynamic-slice_bitcast_fusion.4 = bf16[1024,256]{1,0:T(8,128)(2,1)} fusion(bf16[2,1024,256]{2,1,0:T(8,128)(2,1)} %get-tuple-element.464, s32[]{:T(128)} %get-tuple-element.446), kind=kLoop, calls=%fused_computation.18.clone.1 | loop fusion | bytes 1048580 | tf_op jit(solution)/shard_map/while/body/jit(dynamic_index_in_dim)/squeeze | solution.py:71
  66.2 2.5 %fusion.84 = (f32[768]{0:T(1024)S(1)}, f32[1024,768]{1,0:T(8,128)S(1)}) fusion(s32[768]{0:T(1024)S(1)} %slice.183, s32[768]{0:T(1024)S(1)} %slice.184, s32[1024]{0:T(1024)S(1)} %bitcast.138, pred[1024]{0:T(1024)(128)(4,1)S(1)} %dynamic-slice_reduce_fusion.4, bf16[768,128]{1,0:T(8,128)(2,1)S(1)} %get-tuple-element.465, ...), kind=kOutput, calls=%fused_computation.10.clone.1 | convolution fusion | flops 206830848 | bytes 3618816 | tf_op jit(solution)/shard_map/while/body/eval_jaxpr/dot_general | solution.py:40
  68.8 1.6 %fusion.85 = f32[768]{0:T(1024)S(1)} fusion(f32[1024,768]{1,0:T(8,128)S(1)} %get-tuple-element.381, f32[768]{0:T(1024)S(1)} %select_maximum_fusion.4, s32[768]{0:T(1024)S(1)} %slice.183, s32[768]{0:T(1024)S(1)} %slice.184, s32[1024]{0:T(1024)S(1)} %bitcast.139, pred[1024]{0:T(1024)(128)(4,1)S(1)} %dynamic-slice_reduce_fusion.4), kind=kLoop, calls=%fused_computation.15.clone.1 | loop fusion | flops 6290688 | bytes 3163136 | tf_op jit(solution)/shard_map/while/body/eval_jaxpr/reduce_sum | solution.py:51
  70.5 1.6 %fusion.87 = f32[768,128]{1,0:T(8,128)S(1)} fusion(f32[1024,768]{1,0:T(8,128)S(1)} %get-tuple-element.381, f32[768]{0:T(1024)S(1)} %select_maximum_fusion.4, f32[768,128]{1,0:T(8,128)S(1)} %copy-done.6, bf16[1024,256]{1,0:T(8,128)(2,1)S(1)} %copy-done.1, f32[768]{0:T(1024)S(1)} %get-tuple-element.383, pred[]{:T(512)S(6)} %compare.20, ...), kind=kOutput, calls=%fused_computation.17.clone.1 | convolution fusion | flops 207912960 | bytes 4215809 | tf_op jit(solution)/shard_map/while/body/eval_jaxpr/dot_general | solution.py:52
  72.9 1.9 %dynamic-slice_bitcast_fusion.4 = bf16[1024,256]{1,0:T(8,128)(2,1)} fusion(bf16[2,1024,256]{2,1,0:T(8,128)(2,1)} %get-tuple-element.464, s32[]{:T(128)} %get-tuple-element.446), kind=kLoop, calls=%fused_computation.18.clone.1 | loop fusion | bytes 1048580 | tf_op jit(solution)/shard_map/while/body/jit(dynamic_index_in_dim)/squeeze | solution.py:71
  75.3 2.6 %fusion.84 = (f32[768]{0:T(1024)S(1)}, f32[1024,768]{1,0:T(8,128)S(1)}) fusion(s32[768]{0:T(1024)S(1)} %slice.183, s32[768]{0:T(1024)S(1)} %slice.184, s32[1024]{0:T(1024)S(1)} %bitcast.138, pred[1024]{0:T(1024)(128)(4,1)S(1)} %dynamic-slice_reduce_fusion.4, bf16[768,128]{1,0:T(8,128)(2,1)S(1)} %get-tuple-element.465, ...), kind=kOutput, calls=%fused_computation.10.clone.1 | convolution fusion | flops 206830848 | bytes 3618816 | tf_op jit(solution)/shard_map/while/body/eval_jaxpr/dot_general | solution.py:40
  77.9 1.6 %fusion.85 = f32[768]{0:T(1024)S(1)} fusion(f32[1024,768]{1,0:T(8,128)S(1)} %get-tuple-element.381, f32[768]{0:T(1024)S(1)} %select_maximum_fusion.4, s32[768]{0:T(1024)S(1)} %slice.183, s32[768]{0:T(1024)S(1)} %slice.184, s32[1024]{0:T(1024)S(1)} %bitcast.139, pred[1024]{0:T(1024)(128)(4,1)S(1)} %dynamic-slice_reduce_fusion.4), kind=kLoop, calls=%fused_computation.15.clone.1 | loop fusion | flops 6290688 | bytes 3163136 | tf_op jit(solution)/shard_map/while/body/eval_jaxpr/reduce_sum | solution.py:51
  79.5 1.6 %fusion.87 = f32[768,128]{1,0:T(8,128)S(1)} fusion(f32[1024,768]{1,0:T(8,128)S(1)} %get-tuple-element.381, f32[768]{0:T(1024)S(1)} %select_maximum_fusion.4, f32[768,128]{1,0:T(8,128)S(1)} %copy-done.6, bf16[1024,256]{1,0:T(8,128)(2,1)S(1)} %copy-done.1, f32[768]{0:T(1024)S(1)} %get-tuple-element.383, pred[]{:T(512)S(6)} %compare.20, ...), kind=kOutput, calls=%fused_computation.17.clone.1 | convolution fusion | flops 207912960 | bytes 4215809 | tf_op jit(solution)/shard_map/while/body/eval_jaxpr/dot_general | solution.py:52
  82.7 3.2 %gather_fusion.3 = bf16[16,128,256]{2,1,0:T(8,128)(2,1)} fusion(bf16[32,128,256]{2,1,0:T(8,128)(2,1)} %bitcast.134, s32[1024]{0:T(1024)S(1)} %pad_clamp_fusion), kind=kCustom, calls=%fused_computation.3 | custom fusion | bytes 2097216 | tf_op jit(solution)/shard_map/gather | solution.py:120
  85.9 28.8 %while.31 = (s32[]{:T(128)}, f32[768]{0:T(1024)S(1)}, f32[768]{0:T(1024)}, f32[768,128]{1,0:T(8,128)}, pred[2,1024]{1,0:T(4,128)(4,1)}, /*index=5*/s32[2,1024]{1...) while((s32[]{:T(128)}, f32[768]{0:T(1024)S(1)}, ...), condition=%wide.region_10.11_spmd.clone, body=%wide.region_7.10_spmd.clone.sunk | while | flops 421039872 | bytes 17385808 | solution.py:71
  87.3 1.9 %dynamic-slice_bitcast_fusion.5 = bf16[1024,256]{1,0:T(8,128)(2,1)} fusion(bf16[2,1024,256]{2,1,0:T(8,128)(2,1)} %get-tuple-element.428, s32[]{:T(128)} %get-tuple-element.410), kind=kLoop, calls=%fused_computation.41.clone.1 | loop fusion | bytes 1048580 | tf_op jit(solution)/shard_map/while/body/jit(dynamic_index_in_dim)/squeeze | solution.py:71
  90.9 3.2 %fusion.91 = (f32[768]{0:T(1024)}, f32[1024,768]{1,0:T(8,128)S(1)}) fusion(s32[768]{0:T(1024)S(1)} %slice.187, s32[768]{0:T(1024)S(1)} %slice.188, s32[1024]{0:T(1024)S(1)} %bitcast.141, pred[1024]{0:T(1024)(128)(4,1)S(1)} %dynamic-slice_reduce_fusion.5, bf16[768,128]{1,0:T(8,128)(2,1)} %get-tuple-element.429, ...), kind=kOutput, calls=%fused_computation.33.clone.1 | convolution fusion | flops 206830848 | bytes 3618816 | tf_op jit(solution)/shard_map/while/body/eval_jaxpr/dot_general | solution.py:40
  94.9 2.3 %fusion.92 = f32[768]{0:T(1024)S(1)} fusion(f32[1024,768]{1,0:T(8,128)S(1)} %get-tuple-element.395, f32[768]{0:T(1024)S(1)} %select_maximum_fusion.5, s32[768]{0:T(1024)S(1)} %slice.187, s32[768]{0:T(1024)S(1)} %slice.188, s32[1024]{0:T(1024)S(1)} %bitcast.142, pred[1024]{0:T(1024)(128)(4,1)} %copy-done.10), kind=kLoop, calls=%fused_computation.38.clone.1 | loop fusion | flops 6290688 | bytes 3163136 | tf_op jit(solution)/shard_map/while/body/eval_jaxpr/reduce_sum | solution.py:51
  97.9 1.6 %fusion.94 = f32[768,128]{1,0:T(8,128)S(1)} fusion(f32[1024,768]{1,0:T(8,128)S(1)} %get-tuple-element.395, f32[768]{0:T(1024)S(1)} %select_maximum_fusion.5, f32[768,128]{1,0:T(8,128)S(1)} %copy-done.4, bf16[1024,256]{1,0:T(8,128)(2,1)S(1)} %copy-done.2, f32[768]{0:T(1024)S(1)} %get-tuple-element.397, pred[]{:T(512)S(6)} %compare.21, ...), kind=kOutput, calls=%fused_computation.40.clone.1 | convolution fusion | flops 207912960 | bytes 4215809 | tf_op jit(solution)/shard_map/while/body/eval_jaxpr/dot_general | solution.py:52
  101.7 1.9 %dynamic-slice_bitcast_fusion.5 = bf16[1024,256]{1,0:T(8,128)(2,1)} fusion(bf16[2,1024,256]{2,1,0:T(8,128)(2,1)} %get-tuple-element.428, s32[]{:T(128)} %get-tuple-element.410), kind=kLoop, calls=%fused_computation.41.clone.1 | loop fusion | bytes 1048580 | tf_op jit(solution)/shard_map/while/body/jit(dynamic_index_in_dim)/squeeze | solution.py:71
  105.4 3.2 %fusion.91 = (f32[768]{0:T(1024)}, f32[1024,768]{1,0:T(8,128)S(1)}) fusion(s32[768]{0:T(1024)S(1)} %slice.187, s32[768]{0:T(1024)S(1)} %slice.188, s32[1024]{0:T(1024)S(1)} %bitcast.141, pred[1024]{0:T(1024)(128)(4,1)S(1)} %dynamic-slice_reduce_fusion.5, bf16[768,128]{1,0:T(8,128)(2,1)} %get-tuple-element.429, ...), kind=kOutput, calls=%fused_computation.33.clone.1 | convolution fusion | flops 206830848 | bytes 3618816 | tf_op jit(solution)/shard_map/while/body/eval_jaxpr/dot_general | solution.py:40
  109.3 2.3 %fusion.92 = f32[768]{0:T(1024)S(1)} fusion(f32[1024,768]{1,0:T(8,128)S(1)} %get-tuple-element.395, f32[768]{0:T(1024)S(1)} %select_maximum_fusion.5, s32[768]{0:T(1024)S(1)} %slice.187, s32[768]{0:T(1024)S(1)} %slice.188, s32[1024]{0:T(1024)S(1)} %bitcast.142, pred[1024]{0:T(1024)(128)(4,1)} %copy-done.10), kind=kLoop, calls=%fused_computation.38.clone.1 | loop fusion | flops 6290688 | bytes 3163136 | tf_op jit(solution)/shard_map/while/body/eval_jaxpr/reduce_sum | solution.py:51
  112.3 1.6 %fusion.94 = f32[768,128]{1,0:T(8,128)S(1)} fusion(f32[1024,768]{1,0:T(8,128)S(1)} %get-tuple-element.395, f32[768]{0:T(1024)S(1)} %select_maximum_fusion.5, f32[768,128]{1,0:T(8,128)S(1)} %copy-done.4, bf16[1024,256]{1,0:T(8,128)(2,1)S(1)} %copy-done.2, f32[768]{0:T(1024)S(1)} %get-tuple-element.397, pred[]{:T(512)S(6)} %compare.21, ...), kind=kOutput, calls=%fused_computation.40.clone.1 | convolution fusion | flops 207912960 | bytes 4215809 | tf_op jit(solution)/shard_map/while/body/eval_jaxpr/dot_general | solution.py:52
  121.0 2.2 %divide_convert_fusion = bf16[256,768]{1,0:T(8,128)(2,1)} fusion(f32[256,768]{1,0:T(8,128)} %concatenate.28, f32[256,768]{1,0:T(8,128)} %copy.51), kind=kLoop, calls=%fused_computation.56 | loop fusion | flops 393216 | bytes 1966080 | tf_op jit(solution)/shard_map/convert_element_type | solution.py:143
  (159 shorter events, 36.3 us)
Async XLA Ops:
  7.2 49.1 %all-gather.3.cloned.1.call-start = ((), (), s32[]{:S(2)}) async-start(), calls=%async_computation | async-start | bytes 2228224 | tf_op jit(solution)/shard_map/all_gather | solution.py:107
  15.4 28.3 %copy-start.15 = (s32[32]{0:T(128)S(1)}, s32[32]{0:T(128)}, u32[]{:S(2)}) copy-start(s32[32]{0:T(128)} %param.15) | copy-start | bytes 388
  41.4 2.2 %copy-start.12 = (s32[32]{0:T(128)}, s32[32]{0:T(128)S(1)}, u32[]{:S(2)}) copy-start(s32[32]{0:T(128)S(1)} %and_select_fusion) | copy-start | bytes 388
  59.5 4.3 %copy-start = (bf16[4096,256]{1,0:T(8,128)(2,1)}, bf16[4096,256]{1,0:T(8,128)(2,1)S(1)}, u32[]{:S(2)}) copy-start(bf16[4096,256]{1,0:T(8,128)(2,1)S(1)} %copy.53) | copy-start | bytes 6291460
  68.8 1.7 %copy-start.1 = (bf16[1024,256]{1,0:T(8,128)(2,1)S(1)}, bf16[1024,256]{1,0:T(8,128)(2,1)}, u32[]{:S(2)}) copy-start(bf16[1024,256]{1,0:T(8,128)(2,1)} %dynamic-slice_bitcast_fusion.4) | copy-start | bytes 1572868 | tf_op jit(solution)/shard_map/while
  68.8 1.7 %copy-start.6 = (f32[768,128]{1,0:T(8,128)S(1)}, f32[768,128]{1,0:T(8,128)}, u32[]{:S(2)}) copy-start(f32[768,128]{1,0:T(8,128)} %get-tuple-element.449) | copy-start | bytes 1179652 | tf_op jit(solution)/shard_map/while
  72.1 0.8 copy-start.7
  77.8 1.7 %copy-start.1 = (bf16[1024,256]{1,0:T(8,128)(2,1)S(1)}, bf16[1024,256]{1,0:T(8,128)(2,1)}, u32[]{:S(2)}) copy-start(bf16[1024,256]{1,0:T(8,128)(2,1)} %dynamic-slice_bitcast_fusion.4) | copy-start | bytes 1572868 | tf_op jit(solution)/shard_map/while
  77.8 1.7 %copy-start.6 = (f32[768,128]{1,0:T(8,128)S(1)}, f32[768,128]{1,0:T(8,128)}, u32[]{:S(2)}) copy-start(f32[768,128]{1,0:T(8,128)} %get-tuple-element.449) | copy-start | bytes 1179652 | tf_op jit(solution)/shard_map/while
  81.1 0.8 copy-start.7
  87.3 3.7 %copy-start.10 = (pred[1024]{0:T(1024)(128)(4,1)}, pred[1024]{0:T(1024)(128)(4,1)S(1)}, u32[]{:S(2)}) copy-start(pred[1024]{0:T(1024)(128)(4,1)S(1)} %dynamic-slice_reduce_fusion.5) | copy-start | bytes 3076 | tf_op jit(solution)/shard_map/while
  94.2 3.7 %copy-start.4 = (f32[768,128]{1,0:T(8,128)S(1)}, f32[768,128]{1,0:T(8,128)}, u32[]{:S(2)}) copy-start(f32[768,128]{1,0:T(8,128)} %get-tuple-element.413) | copy-start | bytes 1179652 | tf_op jit(solution)/shard_map/while
  94.2 3.1 %copy-start.8 = (f32[768]{0:T(1024)S(1)}, f32[768]{0:T(1024)}, u32[]{:S(2)}) copy-start(f32[768]{0:T(1024)} %get-tuple-element.412) | copy-start | bytes 9220 | tf_op jit(solution)/shard_map/while
  94.2 3.7 %copy-start.2 = (bf16[1024,256]{1,0:T(8,128)(2,1)S(1)}, bf16[1024,256]{1,0:T(8,128)(2,1)}, u32[]{:S(2)}) copy-start(bf16[1024,256]{1,0:T(8,128)(2,1)} %dynamic-slice_bitcast_fusion.5) | copy-start | bytes 1572868 | tf_op jit(solution)/shard_map/while
  94.2 3.7 %copy-start.11 = (pred[1024]{0:T(1024)(128)(4,1)S(1)}, pred[1024]{0:T(1024)(128)(4,1)}, u32[]{:S(2)}) copy-start(pred[1024]{0:T(1024)(128)(4,1)} %copy-done.10) | copy-start | bytes 3076 | tf_op jit(solution)/shard_map/while
  99.5 0.7 copy-start.5
  101.7 3.7 %copy-start.10 = (pred[1024]{0:T(1024)(128)(4,1)}, pred[1024]{0:T(1024)(128)(4,1)S(1)}, u32[]{:S(2)}) copy-start(pred[1024]{0:T(1024)(128)(4,1)S(1)} %dynamic-slice_reduce_fusion.5) | copy-start | bytes 3076 | tf_op jit(solution)/shard_map/while
  108.6 3.7 %copy-start.4 = (f32[768,128]{1,0:T(8,128)S(1)}, f32[768,128]{1,0:T(8,128)}, u32[]{:S(2)}) copy-start(f32[768,128]{1,0:T(8,128)} %get-tuple-element.413) | copy-start | bytes 1179652 | tf_op jit(solution)/shard_map/while
  108.6 3.1 %copy-start.8 = (f32[768]{0:T(1024)S(1)}, f32[768]{0:T(1024)}, u32[]{:S(2)}) copy-start(f32[768]{0:T(1024)} %get-tuple-element.412) | copy-start | bytes 9220 | tf_op jit(solution)/shard_map/while
  108.6 3.7 %copy-start.2 = (bf16[1024,256]{1,0:T(8,128)(2,1)S(1)}, bf16[1024,256]{1,0:T(8,128)(2,1)}, u32[]{:S(2)}) copy-start(bf16[1024,256]{1,0:T(8,128)(2,1)} %dynamic-slice_bitcast_fusion.5) | copy-start | bytes 1572868 | tf_op jit(solution)/shard_map/while
  108.6 3.7 %copy-start.11 = (pred[1024]{0:T(1024)(128)(4,1)S(1)}, pred[1024]{0:T(1024)(128)(4,1)}, u32[]{:S(2)}) copy-start(pred[1024]{0:T(1024)(128)(4,1)} %copy-done.10) | copy-start | bytes 3076 | tf_op jit(solution)/shard_map/while
  114.7 5.2 %copy-start.3 = (bf16[32,32768]{1,0:T(8,128)(2,1)S(1)}, bf16[32,32768]{1,0:T(8,128)(2,1)}, u32[]{:S(2)}) copy-start(bf16[32,32768]{1,0:T(8,128)(2,1)} %reshape.328) | copy-start | bytes 6291460
  114.7 5.2 %copy-start.13 = (s32[32]{0:T(128)S(1)}, s32[32]{0:T(128)}, u32[]{:S(2)}) copy-start(s32[32]{0:T(128)} %copy-done.12) | copy-start | bytes 388
  114.7 5.2 %copy-start.14 = (s32[2]{0:T(128)S(1)}, s32[2]{0:T(128)}, u32[]{:S(2)}) copy-start(s32[2]{0:T(128)} %fusion.50) | copy-start | bytes 28
  (3 other events, 1.9 us)
Sparse Core Ops, SparseCore 0:
  12.7 43.5 all-gather.2
where the time goes:
time: 131 us; the launch traced here: 130 us
  local copies, waits for them, and re-layouts  43.5 us (33%)
  blocking collectives  23 us (18%)
  other arithmetic  19.2 us (15%)
  matrix products  18.4 us (14%)
  between operations  15.5 us (12%)
  waiting for transfers between devices  10 us (8%)
    all_gather x1, blocking collectives, on_device(): lax.all_gather(tokens, 'seq', axis=0, tiled=True)  23 us
    dot_general x4, matrix products, attend(): jnp.dot(q_rows, kv_block[:, :HD].T, preferred_element_type=jnp.float32)  11.5 us
    all_gather x1, waiting for transfers between devices, on_device(): lax.all_gather(packed, 'seq', axis=0, tiled=True)  10 us
    reduce_sum x4, other arithmetic, attend(): total = total * factor + jnp.sum(weights, axis=1)  7.94 us
    squeeze x4, local copies, waits for them, and re-layouts, sweep(): state, _ = lax.scan(advance, state, items)  7.55 us
    dot_general x4, matrix products, attend(): jnp.dot(weights.astype(jnp.bfloat16), kv_block[:, HD:], preferred_element...  6.42 us
    gather x2, local copies, waits for them, and re-layouts, on_device(): by_span[where_is[jnp.maximum(window, 0)]].reshape(reach * SPAN, 2 * HD)  4.77 us
    unnamed x21, local copies, waits for them, and re-layouts  4.57 us
  transfers between devices with their start and end apart: 1, of which 1 were waited for; matrix products, arithmetic and copies ran while one was open for 7% of the time, Pallas kernels for 0%

commit v1 on v0

v1 whole, which is shorter than its diff:
```python
import functools
import math

import jax
import jax.numpy as jnp
import numpy as np
from jax import lax
from jax.experimental import pallas as pl
from jax.experimental.pallas import tpu as pltpu
from jax.sharding import PartitionSpec as P

HD = 128
QH = 6
SPAN = 128
THETA = 1000000.0
NEG = -1e30
MESH = pl.DeviceIdType.MESH
VMEM = pltpu.VMEM
SMEM = pltpu.SMEM


def tables(span_total):
    half = HD // 2
    freq = (THETA ** (-(np.arange(half) * 2.0 / HD))).astype(np.float32).astype(np.float64)
    sign = np.concatenate([-np.ones(half), np.ones(half)])

    def pair(places):
        angle = np.tile(places[:, None] * freq[None, :], (1, 2))
        return np.stack([np.cos(angle), np.sin(angle) * sign]).astype(np.float32)

    near = pair(np.arange(SPAN, dtype=np.float64))
    far = pair(np.arange(span_total, dtype=np.float64) * SPAN).transpose(1, 0, 2)
    return near, np.ascontiguousarray(far)


def start_of(span, lengths, count):
    ends = jnp.int32(0)
    start = jnp.int32(0)
    for i in range(count):
        size = lengths[i]
        ends = ends + size
        start = start + jnp.where(ends <= span, size, 0)
    return start


def layout_of(n):
    cores = 2 if n % 2 == 0 else 1
    chips = n // cores
    wide = 1
    while (wide + 1) ** 3 <= chips:
        wide += 1
    while chips % wide:
        wide -= 1
    return cores, wide, chips // wide


def gather_kernel(
    n, per_rank, histories,
    span_ids, lengths, near, far, queries, keys, values,
    kv, meta, q_rot,
    send_sem, recv_sem,
):
    cores, wide, deep = layout_of(n)
    me = lax.axis_index("seq")
    group = lax.axis_index("groups")
    c = lax.rem(me, cores)
    x = lax.rem(me // cores, wide)
    z = me // (cores * wide)
    items = per_rank + 1

    def at(zz, xx):
        return (zz * wide + xx) * cores + c

    barrier = pltpu.get_barrier_semaphore()
    neighbours = [
        (z < deep - 1, me + wide * cores),
        (z > 0, me - wide * cores),
        (x < wide - 1, me + cores),
        (x > 0, me - cores),
    ]
    if cores == 2:
        neighbours.append((None, me + 1 - 2 * c))
    greeted = jnp.int32(0)
    for there, other in neighbours:
        def greet(other=other):
            pl.semaphore_signal(barrier, inc=1, device_id=(group, other), device_id_type=MESH)
        if there is None:
            greet()
            greeted = greeted + 1
        else:
            pl.when(there)(greet)
            greeted = greeted + there.astype(jnp.int32)

    factors = []
    for slot in range(per_rank):
        span = span_ids[slot]
        place = span - start_of(span, lengths, histories)
        base = far[pl.ds(place, 1)]
        c2, s2 = base[0, 0:1, :], base[0, 1:2, :]
        c1, s1 = near[0], near[1]
        factors.append((c1 * c2 - s1 * s2, s1 * c2 + c1 * s2))

    def rotate(rows, slot):
        cosine, sine = factors[slot]
        rows = rows.astype(jnp.float32)
        return (rows * cosine + pltpu.roll(rows, HD // 2, 1) * sine).astype(jnp.bfloat16)

    lane = lax.broadcasted_iota(jnp.int32, (1, 128), 1)
    note = jnp.zeros((1, 128), jnp.int32)
    for slot in range(per_rank):
        note = jnp.where(lane == slot, span_ids[slot], note)
    meta[me] = note
    for slot in range(per_rank):
        rows = slice(slot * SPAN, (slot + 1) * SPAN)
        kv[me * per_rank + slot, :, HD:] = values[rows, :]
        kv[me * per_rank + slot, :, :HD] = rotate(keys[rows, :], slot)

    pl.semaphore_wait(barrier, greeted)

    def ref_of(device, k):
        return kv.at[device * per_rank + k] if k < per_rank else meta.at[device]

    pending = []

    def both(a, b):
        return a if b is None else (b if a is None else jnp.logical_and(a, b))

    def send(device, k, target, there):
        number = len(pending)
        ref = ref_of(device, k)
        copy = pltpu.make_async_remote_copy(
            src_ref=ref, dst_ref=ref,
            send_sem=send_sem.at[number], recv_sem=recv_sem.at[device * items + k],
            device_id=(group, target), device_id_type=MESH,
        )
        if there is None:
            copy.start()
            pending.append((None, copy))
        else:
            pl.when(there)(copy.start)
            pending.append((there, copy))

    def arrive(device, k, there):
        ref = ref_of(device, k)
        copy = pltpu.make_async_remote_copy(
            src_ref=ref, dst_ref=ref,
            send_sem=send_sem.at[0], recv_sem=recv_sem.at[device * items + k],
            device_id=(group, me), device_id_type=MESH,
        )
        if there is None:
            copy.wait_recv()
        else:
            pl.when(there)(copy.wait_recv)

    def up(device, k, there):
        send(device, k, me + wide * cores, both(there, z < deep - 1))

    def down(device, k, there):
        send(device, k, me - wide * cores, both(there, z > 0))

    def right(device, k, there):
        send(device, k, me + cores, both(there, x < wide - 1))

    def left(device, k, there):
        send(device, k, me - cores, both(there, x > 0))

    def partner(device, k, there):
        if cores == 2:
            send(device, k, me + 1 - 2 * c, there)

    balanced = wide == 2 and deep >= 4
    late = per_rank - 1

    for k in range(items):
        up(me, k, None)
        down(me, k, None)
        right(me, k, None)
        left(me, k, None)
    for k in range(items):
        partner(me, k, None)

    for slot in range(per_rank):
        rows = slice(slot * SPAN, (slot + 1) * SPAN)
        for head in range(QH):
            q_rot[slot, head * SPAN:(head + 1) * SPAN, :] = rotate(
                queries[rows, head * HD:(head + 1) * HD], slot
            )

    for d in range(deep):
        if d < deep - 1:
            far_by = d + 1
            for k in range(items):
                for sign in (-1, 1):
                    row = z + sign * far_by
                    there = row >= 0 if sign < 0 else row < deep
                    device = at(row, x)
                    arrive(device, k, there)
                    (up if sign < 0 else down)(device, k, there)
                    across = there
                    if balanced and far_by == 1:
                        if sign < 0:
                            along = row == 0
                            if k == late:
                                along = jnp.logical_or(along, row == deep - 2)
                        else:
                            along = row == deep - 1
                            if k == late:
                                along = jnp.logical_or(along, row == 1)
                        across = jnp.logical_and(there, jnp.logical_not(along))
                    right(device, k, across)
                    left(device, k, across)
                    partner(device, k, there)
        for k in range(items):
            for sign in ((-1, 1) if d else (1,)):
                row = z + sign * d
                row_there = None if d == 0 else (row >= 0 if sign < 0 else row < deep)
                for e in range(1, wide):
                    for side in (-1, 1):
                        column = x + side * e
                        there = both(row_there, column >= 0 if side < 0 else column < wide)
                        device = at(row, column)
                        arrive(device, k, there)
                        if e < wide - 1:
                            (right if side < 0 else left)(device, k, there)
                        if balanced and d == 0:
                            rise, fall = z == 0, z == deep - 1
                            if k == late:
                                rise = jnp.logical_or(rise, z == deep - 2)
                                fall = jnp.logical_or(fall, z == 1)
                            up(device, k, both(there, rise))
                            down(device, k, both(there, fall))
                        partner(device, k, there)

    if cores == 2:
        def drain(chip, carry):
            device = chip * cores + 1 - c
            for k in range(items):
                arrive(device, k, None)
            return carry

        lax.fori_loop(0, n // cores, drain, 0)
    for there, copy in pending:
        if there is None:
            copy.wait_send()
        else:
            pl.when(there)(copy.wait_send)


def sends_of(n, per_rank):
    cores, wide, deep = layout_of(n)
    items = per_rank + 1
    total = items * 5 + items * 2 * (deep - 1) * 4
    total += items * (2 * deep - 1) * 2 * (wide - 1) * 4
    return total


def attend_kernel(
    per_rank, span_total, histories, tile, axis,
    span_ids, lengths, page_dest, meta, q_rot, kv,
    context, paged,
    where_is, scores, best, total, accum,
):
    rank = lax.axis_index(axis)
    devices = span_total // per_rank
    gain = math.log2(math.e) / math.sqrt(HD)

    for device in range(devices):
        for k in range(per_rank):
            where_is[meta[device, 0, k]] = device * per_rank + k

    for slot in range(per_rank):
        wanted = rank * per_rank + slot
        found = jnp.int32(0)
        for j in range(span_total):
            found = jnp.where(page_dest[j] == wanted, j, found)
        paged[slot] = kv[where_is[found]]

    def joined(cur, first, width, columns):
        blocks = [kv[where_is[cur - first - j], :, columns] for j in range(width)]
        return blocks[0] if width == 1 else jnp.concatenate(blocks, axis=0)

    def one(item, carry):
        slot = item // (QH * SPAN // tile)
        row0 = pl.multiple_of(lax.rem(item, QH * SPAN // tile) * tile, tile)
        cur = span_ids[slot]
        behind = cur - start_of(cur, lengths, histories)
        fours = behind // 4
        twos = lax.rem(behind, 4) // 2
        ones = lax.rem(behind, 2)
        query = q_rot[slot, pl.ds(row0, tile), :]

        def dots(first, width):
            return lax.dot_general(
                query, joined(cur, first, width, slice(0, HD)),
                (((1,), (1,)), ((), ())), preferred_element_type=jnp.float32,
            )

        def score(first, width):
            block = dots(first, width)
            top = best[...]
            for j in range(width):
                piece = block[:, j * SPAN:(j + 1) * SPAN]
                scores[first + j] = piece
                top = jnp.maximum(top, piece)
            best[...] = top

        def weigh(first, width, fresh=False):
            top = best[...]
            parts, summed = [], None
            for j in range(width):
                part = jnp.exp2((scores[first + j] - top) * gain)
                summed = part if summed is None else summed + part
                parts.append(part.astype(jnp.bfloat16))
            low = parts[0] if width == 1 else jnp.concatenate(parts, axis=1)
            mixed = jnp.dot(
                low, joined(cur, first, width, slice(HD, 2 * HD)), preferred_element_type=jnp.float32
            )
            if fresh:
                total[...] = summed
                accum[...] = mixed
            else:
                total[...] += summed
                accum[...] += mixed

        def sweep(step):
            def body(i, c):
                step(1 + i * 4, 4)
                return c

            lax.fori_loop(0, fours, body, 0)

            @pl.when(twos == 1)
            def _():
                step(1 + fours * 4, 2)

            @pl.when(ones == 1)
            def _():
                step(1 + fours * 4 + twos * 2, 1)

        own = dots(0, 1)
        row = lax.rem(lax.broadcasted_iota(jnp.int32, (tile, SPAN), 0), SPAN)
        col = lax.broadcasted_iota(jnp.int32, (tile, SPAN), 1)
        own = jnp.where(col <= row, own, NEG)
        scores[0] = own
        best[...] = own
        sweep(score)
        best[...] = jnp.broadcast_to(jnp.max(best[...], axis=1, keepdims=True), (tile, SPAN))
        weigh(0, 1, fresh=True)
        sweep(weigh)
        result = accum[...] / jnp.sum(total[...], axis=1, keepdims=True)
        result = result.astype(jnp.bfloat16)
        rows = pl.ds(pl.multiple_of(slot * SPAN, SPAN), SPAN)
        heads = tile // SPAN
        if heads == QH:
            for head in range(QH):
                context[rows, head * HD:(head + 1) * HD] = result[head * SPAN:(head + 1) * SPAN]
        else:
            for head in range(heads):
                place = pl.ds(pl.multiple_of(row0 // SPAN * HD + head * HD, HD), HD)
                context[rows, place] = result[head * SPAN:(head + 1) * SPAN]
        return carry

    lax.fori_loop(0, per_rank * (QH * SPAN // tile), one, 0)


def on_device(n, queries, keys, values, span_ids, lengths, page_dest):
    per_rank = span_ids.shape[0]
    span_total = page_dest.shape[0]
    histories = lengths.shape[0]
    near, far = tables(span_total)
    vmem, smem = pl.BlockSpec(memory_space=VMEM), pl.BlockSpec(memory_space=SMEM)
    items = per_rank + 1
    kv, meta, q_rot = pl.pallas_call(
        functools.partial(gather_kernel, n, per_rank, histories),
        out_shape=(
            jax.ShapeDtypeStruct((span_total, SPAN, 2 * HD), jnp.bfloat16),
            jax.ShapeDtypeStruct((n, 1, 128), jnp.int32),
            jax.ShapeDtypeStruct((per_rank, QH * SPAN, HD), jnp.bfloat16),
        ),
        in_specs=[smem, smem] + [vmem] * 5,
        out_specs=(vmem, vmem, vmem),
        scratch_shapes=[
            pltpu.SemaphoreType.DMA((sends_of(n, per_rank),)),
            pltpu.SemaphoreType.DMA((n * items,)),
        ],
        compiler_params=pltpu.CompilerParams(collective_id=0, has_side_effects=True),
        name="gather",
    )(span_ids, lengths, jnp.asarray(near), jnp.asarray(far), queries, keys, values)
    reach = span_total // 2
    tile = QH * SPAN
    for parts in (1, 2, 3, 6):
        tile = QH * SPAN // parts
        if tile * reach * SPAN * 4 <= 16 * 2**20:
            break
    return pl.pallas_call(
        functools.partial(attend_kernel, per_rank, span_total, histories, tile, "seq"),
        out_shape=(
            jax.ShapeDtypeStruct(queries.shape, jnp.bfloat16),
            jax.ShapeDtypeStruct((per_rank, SPAN, 2 * HD), jnp.bfloat16),
        ),
        in_specs=[smem, smem, smem, smem, vmem, vmem],
        out_specs=(vmem, vmem),
        scratch_shapes=[
            SMEM((span_total,), jnp.int32),
            VMEM((reach, tile, SPAN), jnp.float32),
            VMEM((tile, SPAN), jnp.float32),
            VMEM((tile, SPAN), jnp.float32),
            VMEM((tile, HD), jnp.float32),
        ],
        name="attend",
    )(span_ids, lengths, page_dest, meta, q_rot, kv)


def solution(mesh):
    rows = P(("groups", "seq"), None)
    return jax.shard_map(
        functools.partial(on_device, mesh.shape["seq"]),
        mesh=mesh,
        in_specs=(rows, rows, rows, P(("groups", "seq")), P("groups"), P("groups")),
        out_specs=(rows, P(("groups", "seq"), None, None)),
        check_vma=False,
    )
```

time: 131 us -> 33.6 us (0.26)
  local copies, waits for them, and re-layouts: 43.5 us -> 0 us
  Pallas kernels: 0 us -> 33 us
  blocking collectives: 23 us -> 0 us
  other arithmetic: 19.2 us -> 0 us
  matrix products: 18.4 us -> 0 us
  between operations: 15.5 us -> 0.64 us
  waiting for transfers between devices: 10 us -> 0 us
    pallas_call x0 -> x2, Pallas kernels: none -> 33 us  [the longest x1 25.7 us: on_device(): pl.pallas_call(functools.partial(gather_kernel, n, per_rank, histories),...]
    all_gather x1 -> x0, blocking collectives: 23 us -> none  [on_device(): lax.all_gather(tokens, 'seq', axis=0, tiled=True)]
    dot_general x9 -> x0, matrix products: 18.4 us -> none  [the longest x4 11.5 us: attend(): jnp.dot(q_rows, kv_block[:, :HD].T, preferred_element_type=jnp.float32)]
    all_gather x1 -> x0, waiting for transfers between devices: 10 us -> none  [on_device(): lax.all_gather(packed, 'seq', axis=0, tiled=True)]
    reduce_sum x7 -> x0, other arithmetic: 9.49 us -> none  [the longest x4 7.94 us: attend(): total = total * factor + jnp.sum(weights, axis=1)]
    squeeze x4 -> x0, local copies, waits for them, and re-layouts: 7.55 us -> none  [sweep(): state, _ = lax.scan(advance, state, items)]
    gather x4 -> x0, local copies, waits for them, and re-layouts: 6.09 us -> none  [the longest x2 4.77 us: on_device(): by_span[where_is[jnp.maximum(window, 0)]].reshape(reach * SPAN, 2 * HD)]
    reshape x2 -> x0, local copies, waits for them, and re-layouts: 5.97 us -> none  [the longest x1 3.27 us: on_device(): by_span = whole_kv.reshape(span_total, SPAN, 2 * HD)]
  transfers between devices with their start and end apart: 1 -> 0, of which waited for: 1 -> 0; matrix products, arithmetic and copies ran while one was open for 7% -> 0% of each run, Pallas kernels for 0% -> 0%
where the time goes in v1:
time: 33.6 us; the launch traced here: 33.7 us
  Pallas kernels  33 us (98%)
  between operations  0.64 us (2%)
    pallas_call x1, Pallas kernels, on_device(): pl.pallas_call(functools.partial(gather_kernel, n, per_rank, histories),...  25.7 us
    pallas_call x1, Pallas kernels, on_device(): pl.pallas_call(functools.partial(attend_kernel, per_rank, span_total, his...  7.33 us

profile of v1, /device:TPU:1, one launch (start us, length us, event | category | flops | bytes accessed | tf_op | source)
XLA Modules:
  0.0 33.7 jit_solution(7930375178161334316)
XLA Ops:
  0.6 25.7 %gather.1 = (bf16[32,128,256]{2,1,0:T(8,128)(2,1)}, s32[16,1,128]{2,1,0:T(1,128)}, bf16[2,768,128]{2,1,0:T(8,128)(2,1)}) custom-call(s32[2]{0:T(128)} %span_ids.3, s32[8]{0:T(128)} %lengths.3, f32[2,128,128]{2,1,0:T(8,128)} %constant.4.clone.near, f32[32,2,128]{2,1,0:T(2,128)} %constant.5.clone.far, bf16[256,768]{1,0:T(8,128)(2,1)} %queries.1, ...), custom_call_target="tpu_custom_call" | custom-call | tf_op jit(solution)/shard_map/gather/pallas_call | solution.py:373
  26.3 7.3 %attend.1 = (bf16[256,768]{1,0:T(8,128)(2,1)}, bf16[2,128,256]{2,1,0:T(8,128)(2,1)}) custom-call(s32[2]{0:T(128)} %span_ids.3, s32[8]{0:T(128)} %lengths.3, s32[32]{0:T(128)} %page_dest.1, s32[16,1,128]{2,1,0:T(1,128)} %get-tuple-element.5.meta, bf16[2,768,128]{2,1,0:T(8,128)(2,1)} %get-tuple-element.6.q_rot, bf16[32,128,256]{2,1,0:T(8,128)(2,1)} %get-tuple-element.7.kv), custom_call_target="tpu_custom_call" | custom-call | tf_op jit(solution)/shard_map/attend/pallas_call | solution.py:395

commit v2 on v1

--- a/solution.py
+++ b/solution.py
@@ -56,9 +56,9 @@
 
 def gather_kernel(
     n, per_rank, histories,
-    span_ids, lengths, near, far, queries, keys, values,
+    span_ids_hbm, lengths_hbm, near_hbm, far_hbm, queries_hbm, keys_hbm, values_hbm,
     kv, meta, q_rot,
-    send_sem, recv_sem,
+    span_ids, lengths, near, far, queries, keys, load_sem, send_sem, recv_sem,
 ):
     cores, wide, deep = layout_of(n)
     me = lax.axis_index("seq")
@@ -70,6 +70,20 @@
 
     def at(zz, xx):
         return (zz * wide + xx) * cores + c
+
+    loads = [
+        pltpu.make_async_copy(src, dst, load_sem.at[i])
+        for i, (src, dst) in enumerate([
+            (span_ids_hbm, span_ids), (lengths_hbm, lengths), (far_hbm, far),
+            (keys_hbm, keys), (near_hbm, near),
+        ] + [
+            (values_hbm.at[pl.ds(slot * SPAN, SPAN)],
+             kv.at[me * per_rank + slot, :, pl.ds(HD, HD)])
+            for slot in range(per_rank)
+        ] + [(queries_hbm, queries)])
+    ]
+    for load in loads:
+        load.start()
 
     barrier = pltpu.get_barrier_semaphore()
     neighbours = [
@@ -91,6 +105,9 @@
             pl.when(there)(greet)
             greeted = greeted + there.astype(jnp.int32)
 
+    for load in loads[:-1]:
+        load.wait()
+
     factors = []
     for slot in range(per_rank):
         span = span_ids[slot]
@@ -112,7 +129,6 @@
     meta[me] = note
     for slot in range(per_rank):
         rows = slice(slot * SPAN, (slot + 1) * SPAN)
-        kv[me * per_rank + slot, :, HD:] = values[rows, :]
         kv[me * per_rank + slot, :, :HD] = rotate(keys[rows, :], slot)
 
     pl.semaphore_wait(barrier, greeted)
@@ -172,13 +188,14 @@
     late = per_rank - 1
 
     for k in range(items):
+        down(me, k, None)
         up(me, k, None)
-        down(me, k, None)
         right(me, k, None)
         left(me, k, None)
     for k in range(items):
         partner(me, k, None)
 
+    loads[-1].wait()
     for slot in range(per_rank):
         rows = slice(slot * SPAN, (slot + 1) * SPAN)
         for head in range(QH):
@@ -190,28 +207,21 @@
         if d < deep - 1:
             far_by = d + 1
             for k in range(items):
-                for sign in (-1, 1):
+                for sign in (1, -1):
                     row = z + sign * far_by
                     there = row >= 0 if sign < 0 else row < deep
                     device = at(row, x)
                     arrive(device, k, there)
                     (up if sign < 0 else down)(device, k, there)
                     across = there
-                    if balanced and far_by == 1:
-                        if sign < 0:
-                            along = row == 0
-                            if k == late:
-                                along = jnp.logical_or(along, row == deep - 2)
-                        else:
-                            along = row == deep - 1
-                            if k == late:
-                                along = jnp.logical_or(along, row == 1)
+                    if balanced and k == late:
+                        along = jnp.logical_or(row == 0, row == deep - 1)
                         across = jnp.logical_and(there, jnp.logical_not(along))
                     right(device, k, across)
                     left(device, k, across)
                     partner(device, k, there)
         for k in range(items):
-            for sign in ((-1, 1) if d else (1,)):
+            for sign in ((1, -1) if d else (1,)):
                 row = z + sign * d
                 row_there = None if d == 0 else (row >= 0 if sign < 0 else row < deep)
                 for e in range(1, wide):
@@ -222,13 +232,11 @@
                         arrive(device, k, there)
                         if e < wide - 1:
                             (right if side < 0 else left)(device, k, there)
-                        if balanced and d == 0:
-                            rise, fall = z == 0, z == deep - 1
-                            if k == late:
-                                rise = jnp.logical_or(rise, z == deep - 2)
-                                fall = jnp.logical_or(fall, z == 1)
-                            up(device, k, both(there, rise))
-                            down(device, k, both(there, fall))
+                        if balanced and k == late:
+                            if d == 0 or sign < 0:
+                                up(device, k, both(there, row == 0))
+                            if d == 0 or sign > 0:
+                                down(device, k, both(there, row == deep - 1))
                         partner(device, k, there)
 
     if cores == 2:
@@ -256,10 +264,18 @@
 
 def attend_kernel(
     per_rank, span_total, histories, tile, axis,
-    span_ids, lengths, page_dest, meta, q_rot, kv,
+    span_ids_hbm, lengths_hbm, page_dest_hbm, meta, q_rot, kv,
     context, paged,
-    where_is, scores, best, total, accum,
+    span_ids, lengths, page_dest, load_sem, where_is, scores, best, total, accum,
 ):
+    loads = [
+        pltpu.make_async_copy(src, dst, load_sem.at[i])
+        for i, (src, dst) in enumerate([
+            (span_ids_hbm, span_ids), (lengths_hbm, lengths), (page_dest_hbm, page_dest),
+        ])
+    ]
+    for load in loads:
+        load.start()
     rank = lax.axis_index(axis)
     devices = span_total // per_rank
     gain = math.log2(math.e) / math.sqrt(HD)
@@ -268,6 +284,8 @@
         for k in range(per_rank):
             where_is[meta[device, 0, k]] = device * per_rank + k
 
+    for load in loads:
+        load.wait()
     for slot in range(per_rank):
         wanted = rank * per_rank + slot
         found = jnp.int32(0)
@@ -363,12 +381,18 @@
     lax.fori_loop(0, per_rank * (QH * SPAN // tile), one, 0)
 
 
+def in_hbm(array):
+    return pltpu.with_memory_space_constraint(array, pltpu.HBM)
+
+
 def on_device(n, queries, keys, values, span_ids, lengths, page_dest):
     per_rank = span_ids.shape[0]
     span_total = page_dest.shape[0]
     histories = lengths.shape[0]
     near, far = tables(span_total)
     vmem, smem = pl.BlockSpec(memory_space=VMEM), pl.BlockSpec(memory_space=SMEM)
+    hbm = pl.BlockSpec(memory_space=pltpu.HBM)
+    gathered = span_total * SPAN * 2 * HD * 2
     items = per_rank + 1
     kv, meta, q_rot = pl.pallas_call(
         functools.partial(gather_kernel, n, per_rank, histories),
@@ -377,15 +401,24 @@
             jax.ShapeDtypeStruct((n, 1, 128), jnp.int32),
             jax.ShapeDtypeStruct((per_rank, QH * SPAN, HD), jnp.bfloat16),
         ),
-        in_specs=[smem, smem] + [vmem] * 5,
+        in_specs=[hbm] * 7,
         out_specs=(vmem, vmem, vmem),
         scratch_shapes=[
+            SMEM(span_ids.shape, jnp.int32),
+            SMEM(lengths.shape, jnp.int32),
+            VMEM(near.shape, jnp.float32),
+            VMEM(far.shape, jnp.float32),
+            VMEM(queries.shape, jnp.bfloat16),
+            VMEM(keys.shape, jnp.bfloat16),
+            pltpu.SemaphoreType.DMA((6 + per_rank,)),
             pltpu.SemaphoreType.DMA((sends_of(n, per_rank),)),
             pltpu.SemaphoreType.DMA((n * items,)),
         ],
-        compiler_params=pltpu.CompilerParams(collective_id=0, has_side_effects=True),
+        compiler_params=pltpu.CompilerParams(
+            collective_id=0, has_side_effects=True, vmem_limit_bytes=gathered + 6 * 2**20
+        ),
         name="gather",
-    )(span_ids, lengths, jnp.asarray(near), jnp.asarray(far), queries, keys, values)
+    )(*map(in_hbm, (span_ids, lengths, jnp.asarray(near), jnp.asarray(far), queries, keys, values)))
     reach = span_total // 2
     tile = QH * SPAN
     for parts in (1, 2, 3, 6):
@@ -398,17 +431,22 @@
             jax.ShapeDtypeStruct(queries.shape, jnp.bfloat16),
             jax.ShapeDtypeStruct((per_rank, SPAN, 2 * HD), jnp.bfloat16),
         ),
-        in_specs=[smem, smem, smem, smem, vmem, vmem],
+        in_specs=[hbm, hbm, hbm, smem, vmem, vmem],
         out_specs=(vmem, vmem),
         scratch_shapes=[
+            SMEM(span_ids.shape, jnp.int32),
+            SMEM(lengths.shape, jnp.int32),
+            SMEM(page_dest.shape, jnp.int32),
+            pltpu.SemaphoreType.DMA((3,)),
             SMEM((span_total,), jnp.int32),
             VMEM((reach, tile, SPAN), jnp.float32),
             VMEM((tile, SPAN), jnp.float32),
             VMEM((tile, SPAN), jnp.float32),
             VMEM((tile, HD), jnp.float32),
         ],
+        compiler_params=pltpu.CompilerParams(vmem_limit_bytes=gathered + 24 * 2**20),
         name="attend",
-    )(span_ids, lengths, page_dest, meta, q_rot, kv)
+    )(*map(in_hbm, (span_ids, lengths, page_dest)), meta, q_rot, kv)
 
 
 def solution(mesh):

time: 33.6 us -> 31.1 us (0.926)
  Pallas kernels: 33 us -> 30.6 us
    pallas_call x1, Pallas kernels: 25.7 us -> 23.7 us  [on_device(): pl.pallas_call(functools.partial(gather_kernel, n, per_rank, histories),...]
    pallas_call x1, Pallas kernels: 7.33 us -> 6.92 us  [on_device(): pl.pallas_call(functools.partial(attend_kernel, per_rank, span_total, his...]
where the time goes in v2:
time: 31.1 us; the launch traced here: 31.3 us
  Pallas kernels  30.6 us (98%)
  between operations  0.64 us (2%)
    pallas_call x1, Pallas kernels, on_device(): pl.pallas_call(functools.partial(gather_kernel, n, per_rank, histories),...  23.7 us
    pallas_call x1, Pallas kernels, on_device(): pl.pallas_call(functools.partial(attend_kernel, per_rank, span_total, his...  6.92 us

profile of v2, /device:TPU:1, one launch (start us, length us, event | category | flops | bytes accessed | tf_op | source)
XLA Modules:
  0.0 31.3 jit_solution(10053741189560533821)
XLA Ops:
  0.6 23.7 %gather.1 = (bf16[32,128,256]{2,1,0:T(8,128)(2,1)S(1)}, s32[16,1,128]{2,1,0:T(1,128)S(1)}, bf16[2,768,128]{2,1,0:T(8,128)(2,1)S(1)}) custom-call(s32[2]{0:T(128)} %span_ids_hbm.3, s32[8]{0:T(128)} %lengths_hbm.3, f32[2,128,128]{2,1,0:T(8,128)} %constant.4.clone.near_hbm, f32[32,2,128]{2,1,0:T(2,128)} %constant.5.clone.far_hbm, bf16[256,768]{1,0:T(8,128)(2,1)} %queries_hbm.1, ...), custom_call_target="tpu_custom_call" | custom-call | tf_op jit(solution)/shard_map/gather/pallas_call | solution.py:397
  24.3 6.9 %attend.1 = (bf16[256,768]{1,0:T(8,128)(2,1)}, bf16[2,128,256]{2,1,0:T(8,128)(2,1)}) custom-call(s32[2]{0:T(128)} %span_ids_hbm.3, s32[8]{0:T(128)} %lengths_hbm.3, s32[32]{0:T(128)} %page_dest_hbm.1, s32[16,1,128]{2,1,0:T(1,128)S(1)} %get-tuple-element.5.meta, bf16[2,768,128]{2,1,0:T(8,128)(2,1)S(1)} %get-tuple-element.6.q_rot, ...), custom_call_target="tpu_custom_call" | custom-call | tf_op jit(solution)/shard_map/attend/pallas_call | solution.py:428
